TPU v7x, 32 devices: a whole 2x2x4 slice. The times are simulated.
32 devices in a mesh: ra: 8 (over y, x, core), dec: 4 (over z).
Axes of the slice: x: 2, y: 2, z: 4, core: 2. Of those that a mesh axis runs over, the one named last changes fastest.
Arguments:
- design: float32 [5, 80, 32, 1024], P(None, None, 'ra', 'dec'), may hold values from -6 to 6
- observed: float32 [80, 32, 1024], P(None, 'ra', 'dec'), may hold values from -6 to 6
- weight: float32 [80, 32, 1024], P(None, 'ra', 'dec'), may hold values from 0.3 to 3
- params: float32 [5, 32, 1024], P(None, 'ra', 'dec'), may hold values from -4 to 4
- offsets: int32 [80, 32, 1024], P(None, 'ra', 'dec'), may hold values from 0 to 8, as said below
- counts: int32 [32, 1024], P('ra', 'dec'), may hold values from 10 to 80, as said below
Outputs:
- new_params: float32 [5, 32, 1024], P(None, 'ra', 'dec')
- reduced_chi: float32 [], replicated
Inputs may be any that keep to these rules, and one draw needn't show every extreme that they name: `offsets`: in the first and the last latitude row of cells no offset steps outside the grid in latitude. `counts`: cells near the middle latitude hold more live observations; the two middle latitude rows hold 80.
All inputs are finite; a program needn't handle non-finite values.
Results may differ from a plain program's by a relative error of at most 0.0003.
Values sent between devices are 32-bit elements; how exact they have to be, the bound alone decides.
A program may use at most 64 MiB of HBM per device.

v0:
```python
import functools

import jax
import jax.numpy as jnp
from jax import lax
from jax.experimental import pallas as pl
from jax.experimental.pallas import tpu as pltpu
from jax.sharding import PartitionSpec as P

LANES = 128
PAIRS = [(p, q) for p in range(5) for q in range(p, 5)]
TERMS = 5 + len(PAIRS)
STEPS = (-1, 0, 1)
PASSES = (
    tuple((PAIRS.index(pair), pair) for pair in ((0, 0), (0, 1), (0, 2), (0, 3), (0, 4))),
    tuple((PAIRS.index(pair), pair) for pair in ((1, 1), (1, 2), (1, 3), (1, 4), (2, 2))),
    tuple((PAIRS.index(pair), pair) for pair in ((2, 3), (2, 4), (3, 3), (3, 4), (4, 4))),
)
MESH = pl.DeviceIdType.MESH


def turn(x, shift, axis):
    shift = shift % x.shape[axis]
    return x if shift == 0 else pltpu.roll(x, shift, axis)


def kernel(
    n_ra, n_dec, cells_ra, chunks, unroll,
    d_hbm, o_hbm, w_hbm, p_hbm, off_hbm, cnt_hbm,
    out_ref, chi_ref,
    d_v, o_v, w_v, off_v, p_v, cnt_v, out_ra, out_col, halo_ra, halo_col, near, bins, own,
    send_ra, recv_ra, send_small, recv_small, stat_ra, stat_dec,
    in_sem, one_sem, halo_send, halo_recv, send_sem, recv_sem, stat_send, stat_recv,
):
    slots = d_v.shape[1]
    rows = p_v.shape[1]
    tiles = rows // cells_ra
    size = slots // chunks
    groups = send_ra.shape[1]
    me_ra, me_dec = lax.axis_index("ra"), lax.axis_index("dec")

    def fetches(c):
        part = pl.ds(c * size, size)
        return [
            pltpu.make_async_copy(w_hbm.at[part], w_v.at[part], in_sem.at[1, c]),
            pltpu.make_async_copy(off_hbm.at[part], off_v.at[part], in_sem.at[2, c]),
            pltpu.make_async_copy(d_hbm.at[:, part], d_v.at[:, part], in_sem.at[0, c]),
        ]

    get_counts = pltpu.make_async_copy(cnt_hbm, cnt_v, one_sem.at[0])
    get_params = pltpu.make_async_copy(p_hbm, p_v, one_sem.at[1])
    get_observed = pltpu.make_async_copy(o_hbm, o_v, one_sem.at[2])
    get_counts.start()
    for c in range(chunks):
        for copy in fetches(c):
            copy.start()
        if c == 0:
            get_params.start()
    get_observed.start()

    def device(step_ra, step_dec):
        return (lax.rem(me_ra + step_ra + n_ra, n_ra), lax.rem(me_dec + step_dec + n_dec, n_dec))

    peers = {(a % n_ra, b % n_dec) for a in STEPS for b in STEPS}
    peers |= {(a, 0) for a in range(n_ra)} | {(0, b) for b in range(n_dec)}
    peers = sorted(peers - {(0, 0)})
    barrier = pltpu.get_barrier_semaphore()
    for peer in peers:
        pl.semaphore_signal(barrier, inc=1, device_id=device(*peer), device_id_type=MESH)

    shape = (rows, LANES)
    row = lax.broadcasted_iota(jnp.int32, shape, 0)
    lane = lax.broadcasted_iota(jnp.int32, shape, 1)
    tile = row // cells_ra
    cell = row - tile * cells_ra
    first_tile, last_tile = tile == 0, tile == tiles - 1
    zero = jnp.zeros(shape, jnp.float32)

    def live_weight(s):
        return jnp.where(s < cnt_v[...], w_v[s], 0.0), off_v[s]

    def run(terms, products, begin, count, start):
        def body(t, sums):
            s = begin + 2 * t
            weight, codes = live_weight(s)
            weight_b, codes_b = live_weight(s + 1)
            values, values_b = products(s, weight), products(s + 1, weight_b)
            same = codes == codes_b
            both = [jnp.where(same, x + y, x) for x, y in zip(values, values_b)]
            sums = list(sums)
            for code in range(9):
                hit, hit_b = codes == code, codes_b == code
                for place in range(len(terms)):
                    at = code * len(terms) + place
                    sums[at] = sums[at] + jnp.where(hit, both[place], jnp.where(hit_b, values_b[place], 0.0))
            return tuple(sums)

        step = next(u for u in (unroll, 2, 1) if (count // 2) % u == 0)
        sums = lax.fori_loop(0, count // 2, body, start, unroll=step)
        for code in range(9):
            for place, term in enumerate(terms):
                bins[code * TERMS + term] = sums[code * len(terms) + place]

    def pair_products(group):
        def products(s, weight):
            scaled = {p: weight * d_v[p, s] for p in {pair[0] for _, pair in group}}
            return [scaled[p] * d_v[q, s] for _, (p, q) in group]
        return products

    def pair_terms(group):
        return [5 + place for place, _ in group]

    def observed_products(s, weight):
        scaled = weight * o_v[s]
        return [scaled * d_v[p, s] for p in range(5)]

    none = tuple(zero for _ in range(45))
    terms = pair_terms(PASSES[0])
    for code in range(9):
        for term in terms:
            bins[code * TERMS + term] = zero
    get_counts.wait()

    def chunk(c, carry):
        for copy in fetches(c):
            copy.wait()
        sums = tuple(bins[code * TERMS + term] for code in range(9) for term in terms)
        run(terms, pair_products(PASSES[0]), c * size, size, sums)
        return carry

    lax.fori_loop(0, chunks, chunk, 0)

    get_params.wait()
    columns = [zero, zero]
    packs = [[zero] * halo_ra.shape[1] for _ in range(2)]
    for p in range(5):
        group, spot = divmod(p, cells_ra)
        value = p_v[p]
        columns[0] = jnp.where((lane == p) & first_tile, turn(value, p, 1), columns[0])
        columns[1] = jnp.where((lane == p) & last_tile, turn(value, p + 1, 1), columns[1])
        packs[0][group] = jnp.where(cell == spot, turn(value, spot, 0), packs[0][group])
        packs[1][group] = jnp.where(cell == spot, turn(value, spot - (cells_ra - 1), 0), packs[1][group])
    for side in range(2):
        out_col[side] = columns[side]
        for group in range(halo_ra.shape[1]):
            out_ra[side, group] = packs[side][group]

    @pl.when(me_dec == 0)
    def _():
        for place in (0, 2, 4):
            recv_small[place] = zero

    @pl.when(me_dec == n_dec - 1)
    def _():
        for place in (1, 3, 5):
            recv_small[place] = zero

    def each(copies, arrives, action):
        for way in STEPS:
            chosen = [copy for copy, step in copies if step == way]
            there = me_dec - way if arrives else me_dec + way

            def act(chosen=chosen):
                for copy in chosen:
                    action(copy)

            if way == 0:
                act()
            else:
                pl.when((there >= 0) & (there < n_dec))(act)

    def start(copies):
        each(copies, False, lambda copy: copy.start())

    def sent(copies):
        each(copies, False, lambda copy: copy.wait_send())

    def arrived_all(copies):
        each(copies, True, lambda copy: copy.wait_recv())

    pl.semaphore_wait(barrier, len(peers))
    around = [(0, 1), (1, 1), (-1, 1), (0, -1), (1, -1), (-1, -1)]
    halo_copies = []
    for side, a in enumerate((1, -1)):
        halo_copies.append((pltpu.make_async_remote_copy(
            src_ref=out_ra.at[side], dst_ref=halo_ra.at[side],
            send_sem=halo_send.at[side], recv_sem=halo_recv.at[side],
            device_id=device(-a, 0), device_id_type=MESH,
        ), 0))
    for place, (a, b) in enumerate(around):
        halo_copies.append((pltpu.make_async_remote_copy(
            src_ref=out_col.at[0 if b == 1 else 1], dst_ref=halo_col.at[place],
            send_sem=halo_send.at[2 + place], recv_sem=halo_recv.at[2 + place],
            device_id=device(-a, -b), device_id_type=MESH,
        ), -b))
    start(halo_copies)
    run(pair_terms(PASSES[1]), pair_products(PASSES[1]), 0, slots, none)
    run(pair_terms(PASSES[2]), pair_products(PASSES[2]), 0, slots, none)
    get_observed.wait()
    arrived_all(halo_copies)

    for p in range(5):
        group, spot = divmod(p, cells_ra)
        value = p_v[p]
        column = {}
        for place, (a, b) in enumerate(around):
            column[a, b] = turn(halo_col[place], -1 - p if b == 1 else -p, 1)
        for a in STEPS:
            if a == 0:
                here, after, before = value, column[0, 1], column[0, -1]
            else:
                edge = cells_ra - 1 if a == 1 else 0
                here = jnp.where(
                    cell == edge, turn(halo_ra[0 if a == 1 else 1, group], edge - spot, 0), turn(value, -a, 0))
                after, before = [
                    jnp.where(cell == edge, turn(column[a, b], a * (cells_ra - 1), 0), turn(column[0, b], -a, 0))
                    for b in (1, -1)
                ]
            up = turn(here, 1, 1)
            up_next = turn(jnp.where(last_tile, before, up), cells_ra, 0)
            down = turn(here, -1, 1)
            down_next = turn(jnp.where(first_tile, after, down), -cells_ra, 0)
            code = 3 * (a + 1)
            near[5 * code + p] = jnp.where(lane == 0, up_next, up)
            near[5 * (code + 1) + p] = here
            near[5 * (code + 2) + p] = jnp.where(lane == LANES - 1, down_next, down)

    def squares(s, chi):
        weight, codes = live_weight(s)
        hits = [codes == code for code in range(8)]
        resid = o_v[s]
        for p in range(5):
            source = near[5 * 8 + p]
            for code in range(8):
                source = jnp.where(hits[code], near[5 * code + p], source)
            resid = resid - d_v[p, s] * source
        return chi + weight * resid * resid

    chi = lax.fori_loop(0, slots, squares, zero, unroll=next(u for u in (unroll, 2, 1) if slots % u == 0))
    chi_sum = jnp.sum(chi, axis=0, keepdims=True)
    live_sum = jnp.sum(cnt_v[...], axis=0, keepdims=True).astype(jnp.float32)
    stat_row = lax.broadcasted_iota(jnp.int32, (2, LANES), 0)
    stat_ra[me_ra] = jnp.where(stat_row == 0, chi_sum, live_sum)

    def stat_copies(buffer, me, count, base, target):
        return [
            pltpu.make_async_remote_copy(
                src_ref=buffer.at[me], dst_ref=buffer.at[me],
                send_sem=stat_send.at[base + step - 1], recv_sem=stat_recv.at[base + step - 1],
                device_id=target(step), device_id_type=MESH,
            )
            for step in range(1, count)
        ]

    along_ra = stat_copies(stat_ra, me_ra, n_ra, 0, lambda step: device(step, 0))
    for copy in along_ra:
        copy.start()
    run(list(range(5)), observed_products, 0, slots, none)
    for copy in along_ra:
        copy.wait_recv()
    stat_dec[me_dec] = functools.reduce(lambda x, y: x + y, [stat_ra[k] for k in range(n_ra)])
    along_dec = stat_copies(stat_dec, me_dec, n_dec, n_ra - 1, lambda step: device(0, step))
    for copy in along_dec:
        copy.start()

    def shift_dec(low, mid, high):
        up = turn(high, 1, 1)
        up_next = turn(up, cells_ra, 0)
        down = turn(low, -1, 1)
        down_next = turn(down, -cells_ra, 0)
        kept = (
            mid
            + jnp.where(lane == 0, jnp.where(first_tile, 0.0, up_next), up)
            + jnp.where(lane == LANES - 1, jnp.where(last_tile, 0.0, down_next), down)
        )
        return kept, up_next, down_next

    def pack_dec(packed, place, up_next, down_next):
        high = jnp.where((lane == place) & first_tile, turn(up_next, place, 1), packed[0])
        low = jnp.where((lane == place) & last_tile, turn(down_next, place + 1, 1), packed[1])
        return high, low

    edge = (zero, zero)
    corners = [(zero, zero), (zero, zero)]
    for group in range(groups):
        packed = [[zero] * 3, [zero] * 3]
        for term in range(group * cells_ra, min(TERMS, (group + 1) * cells_ra)):
            spot = term - group * cells_ra
            merged = []
            for at in range(3):
                down, mid, up = [bins[(3 * a + at) * TERMS + term] for a in range(3)]
                merged.append(
                    mid
                    + jnp.where(cell >= 1, turn(up, 1, 0), 0.0)
                    + jnp.where(cell <= cells_ra - 2, turn(down, -1, 0), 0.0)
                )
                packed[0][at] = jnp.where(cell == spot, turn(up, spot - (cells_ra - 1), 0), packed[0][at])
                packed[1][at] = jnp.where(cell == spot, turn(down, spot, 0), packed[1][at])
            kept, up_next, down_next = shift_dec(*merged)
            own[term] = kept
            edge = pack_dec(edge, term, up_next, down_next)
        for side in range(2):
            kept, up_next, down_next = shift_dec(*packed[side])
            send_ra[side, group] = kept
            corners[side] = pack_dec(corners[side], group, up_next, down_next)
    small = [edge[0], edge[1], corners[0][0], corners[0][1], corners[1][0], corners[1][1]]
    small_steps = [(0, 1), (0, -1), (1, 1), (1, -1), (-1, 1), (-1, -1)]
    for place, value in enumerate(small):
        send_small[place] = value

    copies = []
    for side, step in enumerate((1, -1)):
        copies.append((pltpu.make_async_remote_copy(
            src_ref=send_ra.at[side], dst_ref=recv_ra.at[side],
            send_sem=send_sem.at[side], recv_sem=recv_sem.at[side],
            device_id=device(step, 0), device_id_type=MESH,
        ), 0))
    for place, step in enumerate(small_steps):
        copies.append((pltpu.make_async_remote_copy(
            src_ref=send_small.at[place], dst_ref=recv_small.at[place],
            send_sem=send_sem.at[2 + place], recv_sem=recv_sem.at[2 + place],
            device_id=device(*step), device_id_type=MESH,
        ), step[1]))
    start(copies)
    sent(halo_copies)
    for copy in along_ra:
        copy.wait_send()
    for copy in along_dec:
        copy.wait_recv()
    stats = functools.reduce(lambda x, y: x + y, [stat_dec[k] for k in range(n_dec)])
    chi_ref[0] = jnp.sum(stats[0:1]) / jnp.sum(stats[1:2])
    for copy in along_dec:
        copy.wait_send()
    arrived_all(copies)

    def unpack_dec(pair, place):
        high = jnp.where((lane == 0) & first_tile, turn(pair[0], -place, 1), 0.0)
        low = jnp.where((lane == LANES - 1) & last_tile, turn(pair[1], -(place + 1), 1), 0.0)
        return high + low

    edge = (recv_small[0], recv_small[1])
    total = []
    for group in range(groups):
        arrived = [
            recv_ra[side, group]
            + unpack_dec((recv_small[2 + 2 * side], recv_small[3 + 2 * side]), group)
            for side in range(2)
        ]
        for term in range(group * cells_ra, min(TERMS, (group + 1) * cells_ra)):
            spot = term - group * cells_ra
            total.append(
                own[term]
                + unpack_dec(edge, term)
                + jnp.where(cell == 0, turn(arrived[0], -spot, 0), 0.0)
                + jnp.where(cell == cells_ra - 1, turn(arrived[1], cells_ra - 1 - spot, 0), 0.0)
            )

    params = [p_v[p] for p in range(5)]
    lower = [[None] * 5 for _ in range(5)]
    inverse = [None] * 5
    forward = []
    for q in range(5):
        for p in range(q, 5):
            running = total[5 + PAIRS.index((q, p))]
            if p == q:
                running = running + 1.0
            for inner in range(q):
                running = running - lower[p][inner] * lower[q][inner]
            if p == q:
                inverse[q] = 1.0 / jnp.sqrt(running)
            else:
                lower[p][q] = running * inverse[q]
    for p in range(5):
        running = total[p] + params[p]
        for inner in range(p):
            running = running - lower[p][inner] * forward[inner]
        forward.append(running * inverse[p])
    answer = [None] * 5
    for p in range(4, -1, -1):
        running = forward[p]
        for inner in range(p + 1, 5):
            running = running - lower[inner][p] * answer[inner]
        answer[p] = running * inverse[p]
        out_ref[p] = answer[p]

    sent(copies)


def per_device(n_ra, n_dec, design, observed, weight, params, offsets, counts):
    slots, cells_ra, cells_dec = observed.shape
    tiles = cells_dec // LANES
    rows = tiles * cells_ra

    def fold(x):
        x = x.reshape(x.shape[:-1] + (tiles, LANES))
        return jnp.swapaxes(x, -3, -2).reshape(x.shape[:-3] + (rows, LANES))

    chunks = next(c for c in (4, 2, 1) if slots % (2 * c) == 0)
    unroll = 2
    groups = -(-TERMS // cells_ra)
    anywhere = pl.BlockSpec(memory_space=pl.ANY)
    vmem = pl.BlockSpec(memory_space=pltpu.VMEM)
    new_params, chi = pl.pallas_call(
        functools.partial(kernel, n_ra, n_dec, cells_ra, chunks, unroll),
        out_shape=(
            jax.ShapeDtypeStruct((5, rows, LANES), jnp.float32),
            jax.ShapeDtypeStruct((1,), jnp.float32),
        ),
        in_specs=[anywhere] * 6,
        out_specs=(vmem, pl.BlockSpec(memory_space=pltpu.SMEM)),
        scratch_shapes=[
            pltpu.VMEM((5, slots, rows, LANES), jnp.float32),
            pltpu.VMEM((slots, rows, LANES), jnp.float32),
            pltpu.VMEM((slots, rows, LANES), jnp.float32),
            pltpu.VMEM((slots, rows, LANES), jnp.int32),
            pltpu.VMEM((5, rows, LANES), jnp.float32),
            pltpu.VMEM((rows, LANES), jnp.int32),
            pltpu.VMEM((2, -(-5 // cells_ra), rows, LANES), jnp.float32),
            pltpu.VMEM((2, rows, LANES), jnp.float32),
            pltpu.VMEM((2, -(-5 // cells_ra), rows, LANES), jnp.float32),
            pltpu.VMEM((6, rows, LANES), jnp.float32),
            pltpu.VMEM((45, rows, LANES), jnp.float32),
            pltpu.VMEM((9 * TERMS, rows, LANES), jnp.float32),
            pltpu.VMEM((TERMS, rows, LANES), jnp.float32),
            pltpu.VMEM((2, groups, rows, LANES), jnp.float32),
            pltpu.VMEM((2, groups, rows, LANES), jnp.float32),
            pltpu.VMEM((6, rows, LANES), jnp.float32),
            pltpu.VMEM((6, rows, LANES), jnp.float32),
            pltpu.VMEM((n_ra, 2, LANES), jnp.float32),
            pltpu.VMEM((n_dec, 2, LANES), jnp.float32),
            pltpu.SemaphoreType.DMA((3, chunks)),
            pltpu.SemaphoreType.DMA((3,)),
            pltpu.SemaphoreType.DMA((8,)),
            pltpu.SemaphoreType.DMA((8,)),
            pltpu.SemaphoreType.DMA((8,)),
            pltpu.SemaphoreType.DMA((8,)),
            pltpu.SemaphoreType.DMA((n_ra + n_dec - 2,)),
            pltpu.SemaphoreType.DMA((n_ra + n_dec - 2,)),
        ],
        compiler_params=pltpu.CompilerParams(collective_id=0, has_side_effects=True),
    )(fold(design), fold(observed), fold(weight), fold(params), fold(offsets), fold(counts))
    new_params = jnp.swapaxes(new_params.reshape(5, tiles, cells_ra, LANES), 1, 2)
    return new_params.reshape(params.shape), chi[0]


def solution(mesh):
    return jax.shard_map(
        functools.partial(per_device, mesh.shape["ra"], mesh.shape["dec"]),
        mesh=mesh,
        in_specs=(
            P(None, None, "ra", "dec"),
            P(None, "ra", "dec"),
            P(None, "ra", "dec"),
            P(None, "ra", "dec"),
            P(None, "ra", "dec"),
            P("ra", "dec"),
        ),
        out_specs=(P(None, "ra", "dec"), P()),
        check_vma=False,
    )
```

profile of v0, /device:TPU:0, one launch (start us, length us, event | category | flops | bytes accessed | tf_op | source)
XLA Modules:
  0.0 22.2 jit_solution(9048044683969267556)
XLA Ops:
  0.6 18.5 %shard_map.77 = (f32[5,8,128]{2,1,0:T(8,128)}, f32[1]{0:T(128)}) custom-call(f32[5,80,8,128]{3,2,1,0:T(8,128)} %bitcast.36, f32[80,8,128]{2,1,0:T(8,128)} %bitcast.37, f32[80,8,128]{2,1,0:T(8,128)} %bitcast.38, f32[5,8,128]{2,1,0:T(8,128)} %bitcast.40, s32[80,8,128]{2,1,0:T(8,128)} %bitcast.39, s32[8,128]{1,0:T(8,128)} %bitcast.42), custom_call_target="tpu_custom_call" | custom-call | tf_op jit(solution)/shard_map/pallas_call | solution.py:403
  19.1 1.3 %copy.17 = f32[5,4,256]{2,1,0:T(4,128)} copy(f32[5,4,256]{2,1,0:T(4,128)} %bitcast.41) | data formatting | bytes 40960
where the time goes:
time: 22.5 us; the launch traced here: 22.2 us
  Pallas kernels  18.5 us (82%)
  between operations  2.4 us (11%)
  local copies, waits for them, and re-layouts  1.34 us (6%)
    pallas_call x1, Pallas kernels, per_device(): pl.pallas_call(functools.partial(kernel, n_ra, n_dec, cells_ra, chunks, u...  18.5 us
    unnamed x1, local copies, waits for them, and re-layouts  1.34 us

commit v1 on v0

--- a/solution.py
+++ b/solution.py
@@ -328,7 +328,7 @@
     for copy in along_dec:
         copy.wait_recv()
     stats = functools.reduce(lambda x, y: x + y, [stat_dec[k] for k in range(n_dec)])
-    chi_ref[0] = jnp.sum(stats[0:1]) / jnp.sum(stats[1:2])
+    chi_ref[...] = jnp.full((8,128), jnp.sum(stats[0:1]) / jnp.sum(stats[1:2]))
     for copy in along_dec:
         copy.wait_send()
     arrived_all(copies)
@@ -398,16 +398,16 @@
     chunks = next(c for c in (4, 2, 1) if slots % (2 * c) == 0)
     unroll = 2
     groups = -(-TERMS // cells_ra)
-    anywhere = pl.BlockSpec(memory_space=pl.ANY)
+    anywhere = pl.BlockSpec(memory_space=pltpu.HBM)
     vmem = pl.BlockSpec(memory_space=pltpu.VMEM)
     new_params, chi = pl.pallas_call(
         functools.partial(kernel, n_ra, n_dec, cells_ra, chunks, unroll),
         out_shape=(
             jax.ShapeDtypeStruct((5, rows, LANES), jnp.float32),
-            jax.ShapeDtypeStruct((1,), jnp.float32),
+            jax.ShapeDtypeStruct((8,128), jnp.float32),
         ),
         in_specs=[anywhere] * 6,
-        out_specs=(vmem, pl.BlockSpec(memory_space=pltpu.SMEM)),
+        out_specs=(vmem, vmem),
         scratch_shapes=[
             pltpu.VMEM((5, slots, rows, LANES), jnp.float32),
             pltpu.VMEM((slots, rows, LANES), jnp.float32),
@@ -437,8 +437,21 @@
             pltpu.SemaphoreType.DMA((n_ra + n_dec - 2,)),
             pltpu.SemaphoreType.DMA((n_ra + n_dec - 2,)),
         ],
-        compiler_params=pltpu.CompilerParams(collective_id=0, has_side_effects=True),
-    )(fold(design), fold(observed), fold(weight), fold(params), fold(offsets), fold(counts))
+        compiler_params=pltpu.CompilerParams(collective_id=0, has_side_effects=True, vmem_limit_bytes=16*1024*1024),
+    )(*[pltpu.with_memory_space_constraint(fold(x), pltpu.HBM) for x in (design, observed, weight, params, offsets, counts)])
+    def finish(x_ref, c_ref, out_ref, s_ref):
+        out_ref[...] = x_ref[...]
+        s_ref[0] = c_ref[0, 0]
+    new_params, chi = pl.pallas_call(
+        finish,
+        out_shape=(
+            jax.ShapeDtypeStruct((5, rows, LANES), jnp.float32),
+            jax.ShapeDtypeStruct((1,), jnp.float32),
+        ),
+        in_specs=[vmem, vmem],
+        out_specs=(vmem, pl.BlockSpec(memory_space=pltpu.SMEM)),
+        compiler_params=pltpu.CompilerParams(vmem_limit_bytes=1024*1024),
+    )(new_params, chi)
     new_params = jnp.swapaxes(new_params.reshape(5, tiles, cells_ra, LANES), 1, 2)
     return new_params.reshape(params.shape), chi[0]
 

time: 22.5 us -> 19.3 us (0.86)
  between operations: 2.4 us -> 0.64 us
  local copies, waits for them, and re-layouts: 1.34 us -> 0 us
    unnamed x1 -> x0, local copies, waits for them, and re-layouts: 1.34 us -> none
    pallas_call x1, Pallas kernels: 18.5 us -> 17.9 us  [per_device(): pl.pallas_call(functools.partial(kernel, n_ra, n_dec, cells_ra, chunks, u...]
    pallas_call x0 -> x1, Pallas kernels: none -> 0.62 us  [per_device(): pl.pallas_call(finish, out_shape=(jax.ShapeDtypeStruct((5, rows, LANES),...]
where the time goes in v1:
time: 19.3 us; the launch traced here: 19.1 us
  Pallas kernels  18.5 us (96%)
  between operations  0.64 us (3%)
    pallas_call x1, Pallas kernels, per_device(): pl.pallas_call(functools.partial(kernel, n_ra, n_dec, cells_ra, chunks, u...  17.9 us
    pallas_call x1, Pallas kernels, per_device(): pl.pallas_call(finish, out_shape=(jax.ShapeDtypeStruct((5, rows, LANES),...  0.62 us

profile of v1, /device:TPU:0, one launch (start us, length us, event | category | flops | bytes accessed | tf_op | source)
XLA Modules:
  0.0 19.1 jit_solution(8181756905285160475)
XLA Ops:
  0.6 17.9 %shard_map.77 = (f32[5,8,128]{2,1,0:T(8,128)S(1)}, f32[8,128]{1,0:T(8,128)S(1)}) custom-call(f32[5,80,8,128]{3,2,1,0:T(8,128)} %bitcast.36, f32[80,8,128]{2,1,0:T(8,128)} %bitcast.37, f32[80,8,128]{2,1,0:T(8,128)} %bitcast.38, f32[5,8,128]{2,1,0:T(8,128)} %bitcast.40, s32[80,8,128]{2,1,0:T(8,128)} %bitcast.39, s32[8,128]{1,0:T(8,128)} %bitcast.41), custom_call_target="tpu_custom_call" | custom-call | tf_op jit(solution)/shard_map/pallas_call | solution.py:403
  18.5 0.6 %shard_map.78 = (f32[5,8,128]{2,1,0:T(8,128)}, f32[1]{0:T(128)}) custom-call(f32[5,8,128]{2,1,0:T(8,128)S(1)} %get-tuple-element.6.x_ref, f32[8,128]{1,0:T(8,128)S(1)} %get-tuple-element.7.c_ref), custom_call_target="tpu_custom_call" | custom-call | tf_op jit(solution)/shard_map/pallas_call | solution.py:445

commit v2 on v1

v2 whole, which is shorter than its diff:
```python
import functools

import jax
import jax.numpy as jnp
from jax import lax
from jax.experimental import pallas as pl
from jax.experimental.pallas import tpu as pltpu
from jax.sharding import PartitionSpec as P

LANES = 128
PAIRS = [(p, q) for p in range(5) for q in range(p, 5)]
TERMS = 5 + len(PAIRS)
STEPS = (-1, 0, 1)
GROUPS = (tuple(range(5, 15)), tuple(range(15, TERMS)) + tuple(range(5)))
MESH = pl.DeviceIdType.MESH
QUARTERS = (1, 3)
WIDTH = 4


def turn(x, shift, axis):
    shift = shift % x.shape[axis]
    return x if shift == 0 else pltpu.roll(x, shift, axis)


def kernel(
    n_ra, n_dec, cells_ra, chunks,
    d_hbm, o_hbm, w_hbm, p_hbm, off_hbm, cnt_hbm,
    out_ref, chi_ref,
    data, off_v, p_v, cnt_v, out_ra, out_col, halo_ra, halo_col, near, bins, own,
    send_ra, recv_ra, send_small, recv_small, stat, where_v,
    local_sem, small_sem, send_sem, halo_sem, sums_sem, stat_sem, far_sem,
):
    slots = data.shape[1]
    rows = cnt_v.shape[0]
    tiles = rows // cells_ra
    size = slots // chunks
    groups = send_ra.shape[1]
    me_ra, me_dec = lax.axis_index("ra"), lax.axis_index("dec")
    design, observed, weight = data.at[pl.ds(0, 5)], data.at[5], data.at[6]

    def fetch(c):
        part = pl.ds(c * size, size)
        for source, target in (
            (w_hbm.at[part], weight.at[part]),
            (off_hbm.at[part], off_v.at[part]),
            (d_hbm.at[:, part], design.at[:, part]),
            (o_hbm.at[part], observed.at[part]),
        ):
            pltpu.make_async_copy(source, target, local_sem.at[c]).start()

    def fetched(c):
        part = data.at[:, pl.ds(c * size, size)]
        pltpu.make_async_copy(part, part, local_sem.at[c]).wait()

    pltpu.make_async_copy(cnt_hbm, cnt_v, small_sem.at[0]).start()
    pltpu.make_async_copy(p_hbm, p_v.at[pl.ds(0, 5)], small_sem.at[0]).start()
    fetch(0)

    def device(step_ra, step_dec):
        return (lax.rem(me_ra + step_ra + n_ra, n_ra), lax.rem(me_dec + step_dec + n_dec, n_dec))

    def everyone(action):
        decs = [lax.rem(me_dec + b, n_dec) for b in range(n_dec)]
        for b in range(1, n_dec):
            action((me_ra, decs[b]))

        def group(a, carry):
            there = lax.rem(me_ra + a, n_ra)
            for dec in decs:
                action((there, dec))
            return carry

        lax.fori_loop(1, n_ra, group, 0, unroll=n_ra * n_dec <= 64)

    def signal(sem, target):
        pl.semaphore_signal(sem, inc=1, device_id=target, device_id_type=MESH)

    aside = sorted({1 % n_ra, -1 % n_ra} - {0})
    lines = [(a, 0) for a in range(1, n_ra)] + [(0, b) for b in range(1, n_dec)]
    corners_of = [(me_dec + b, [(a, b) for a in aside]) for b in (1, -1)]
    barrier = pltpu.get_barrier_semaphore()
    greeted = len(lines)
    for dec, peers in corners_of:
        inside = (dec >= 0) & (dec < n_dec)
        greeted = greeted + len(aside) * inside.astype(jnp.int32)

        def greet(peers=peers):
            for peer in peers:
                signal(barrier, device(*peer))

        pl.when(inside)(greet)
    for peer in lines:
        signal(barrier, device(*peer))
    for c in range(1, chunks):
        fetch(c)

    shape = (rows, LANES)
    row = lax.broadcasted_iota(jnp.int32, shape, 0)
    where_v[0] = lax.broadcasted_iota(jnp.int32, shape, 1)
    where_v[1] = row // cells_ra
    where_v[2] = row - where_v[1] * cells_ra

    def position():
        lane, tile, cell = where_v[0], where_v[1], where_v[2]
        return lane, cell, tile == 0, tile == tiles - 1

    zero = jnp.zeros(shape, jnp.float32)

    def clear(at, carry):
        bins[at] = zero
        return carry

    lax.fori_loop(0, 9 * TERMS, clear, 0, unroll=6)
    pltpu.make_async_copy(p_v, p_v, small_sem.at[0]).wait()
    pairs = 2 if size % 4 == 0 else 1

    def products(group, s, scale):
        d = [design[p, s] for p in range(5)]
        scaled = {}

        def by(p):
            if p not in scaled:
                scaled[p] = scale * (observed[s] if p == 5 else d[p])
            return scaled[p]

        return [by(5) * d[term] if term < 5 else by(PAIRS[term - 5][0]) * d[PAIRS[term - 5][1]] for term in group]

    def accumulate(begin, carry):
        def body(t, carry):
            first = begin + 2 * pairs * t
            codes, scales = [], []
            for k in range(2 * pairs):
                scale = jnp.where(first + k < cnt_v[...], weight[first + k], 0.0)
                scales.append(scale)
                codes.append(off_v[first + k])
            same = [codes[2 * k] == codes[2 * k + 1] for k in range(pairs)]
            for group in GROUPS:
                values = [products(group, first + k, scales[k]) for k in range(2 * pairs)]
                both = [
                    [jnp.where(same[k], x + y, x) for x, y in zip(values[2 * k], values[2 * k + 1])]
                    for k in range(pairs)
                ]
                for code in range(9):
                    hits = [c == code for c in codes]
                    for place, term in enumerate(group):
                        total = bins[code * TERMS + term]
                        for k in range(pairs):
                            second = jnp.where(hits[2 * k + 1], values[2 * k + 1][place], 0.0)
                            total = total + jnp.where(hits[2 * k], both[k][place], second)
                        bins[code * TERMS + term] = total
            return carry

        return lax.fori_loop(0, size // (2 * pairs), body, carry)

    def chunk(c, carry):
        fetched(c)
        return accumulate(c * size, carry)

    ends = [-(-chunks * quarter // 4) for quarter in QUARTERS]
    lax.fori_loop(0, ends[0], chunk, 0)

    lane, cell, first_tile, last_tile = position()
    columns = [zero, zero]
    packs = [[zero] * halo_ra.shape[1] for _ in range(2)]
    for p in range(5):
        group, spot = divmod(p, cells_ra)
        value = p_v[p]
        columns[0] = jnp.where((lane == p) & first_tile, turn(value, p, 1), columns[0])
        columns[1] = jnp.where((lane == p) & last_tile, turn(value, p + 1, 1), columns[1])
        packs[0][group] = jnp.where(cell == spot, turn(value, spot, 0), packs[0][group])
        packs[1][group] = jnp.where(cell == spot, turn(value, spot - (cells_ra - 1), 0), packs[1][group])
    for side in range(2):
        out_col[side] = columns[side]
        for group in range(halo_ra.shape[1]):
            out_ra[side, group] = packs[side][group]

    @pl.when(me_dec == 0)
    def _():
        for place in range(0, 3):
            recv_small[place] = zero

    @pl.when(me_dec == n_dec - 1)
    def _():
        for place in range(3, 6):
            recv_small[place] = zero

    def each(arrives, action):
        for way in STEPS:
            there = me_dec - way if arrives else me_dec + way
            if way == 0:
                action(way)
            else:
                pl.when((there >= 0) & (there < n_dec))(functools.partial(action, way))

    def await_bytes(ref, sem):
        pltpu.make_async_copy(ref, ref, sem).wait()

    def remote(source, target, sem, way, step_ra):
        pltpu.make_async_remote_copy(
            src_ref=source, dst_ref=target, send_sem=send_sem.at[way + 1], recv_sem=sem.at[way + 1],
            device_id=device(step_ra, way), device_id_type=MESH,
        ).start()

    pl.semaphore_wait(barrier, greeted)
    around = {1: [(0, 1), (1, 1), (-1, 1)], -1: [(0, -1), (1, -1), (-1, -1)]}
    places = around[1] + around[-1]

    def send_halo(way):
        if way == 0:
            for side, a in enumerate((1, -1)):
                remote(out_ra.at[side], halo_ra.at[side], halo_sem, 0, -a)
        for a, b in around.get(-way, []):
            remote(out_col.at[0 if b == 1 else 1], halo_col.at[places.index((a, b))], halo_sem, way, -a)

    def halo_side(ref, way):
        return ref.at[pl.ds(0 if way == -1 else 3, 3)]

    each(False, send_halo)
    for b in range(1, n_dec):
        signal(far_sem, device(0, b))
    lax.fori_loop(ends[0], ends[1], chunk, 0)
    for c in range(ends[1], chunks):
        fetched(c)
    each(True, lambda way: await_bytes(halo_side(halo_col, way) if way else halo_ra, halo_sem.at[way + 1]))
    around = places
    lane, cell, first_tile, last_tile = position()

    for p in range(5):
        group, spot = divmod(p, cells_ra)
        value = p_v[p]
        column = {}
        for place, (a, b) in enumerate(around):
            column[a, b] = turn(halo_col[place], -1 - p if b == 1 else -p, 1)
        for a in STEPS:
            if a == 0:
                here, after, before = value, column[0, 1], column[0, -1]
            else:
                edge = cells_ra - 1 if a == 1 else 0
                here = jnp.where(
                    cell == edge, turn(halo_ra[0 if a == 1 else 1, group], edge - spot, 0), turn(value, -a, 0))
                after, before = [
                    jnp.where(cell == edge, turn(column[a, b], a * (cells_ra - 1), 0), turn(column[0, b], -a, 0))
                    for b in (1, -1)
                ]
            up = turn(here, 1, 1)
            up_next = turn(jnp.where(last_tile, before, up), cells_ra, 0)
            down = turn(here, -1, 1)
            down_next = turn(jnp.where(first_tile, after, down), -cells_ra, 0)
            code = 3 * (a + 1)
            near[5 * code + p] = jnp.where(lane == 0, up_next, up)
            near[5 * (code + 1) + p] = here
            near[5 * (code + 2) + p] = jnp.where(lane == LANES - 1, down_next, down)

    width = next(u for u in (WIDTH, 2, 1) if slots % u == 0)

    tables = [[near[5 * code + p] for code in range(9)] for p in range(5)]

    def squares(t, chi):
        chosen = []
        for s in range(width):
            codes = off_v[t * width + s]
            low, middle = codes < 3, codes < 6
            codes = codes - jnp.where(low, 0, jnp.where(middle, 3, 6))
            chosen.append((low, middle, codes < 1, codes < 2))
        resids = [observed[t * width + s] for s in range(width)]
        scales = [jnp.where(t * width + s < cnt_v[...], weight[t * width + s], 0.0) for s in range(width)]
        for p in range(5):
            table = tables[p]
            for s, (low, middle, left, centre) in enumerate(chosen):
                row = [jnp.where(low, table[b], jnp.where(middle, table[3 + b], table[6 + b])) for b in range(3)]
                source = jnp.where(left, row[0], jnp.where(centre, row[1], row[2]))
                resids[s] = resids[s] - design[p, t * width + s] * source
        return tuple(x + scales[s] * r * r for s, (x, r) in enumerate(zip(chi, resids)))

    chi = lax.fori_loop(0, slots // width, squares, (zero,) * width)
    chi = functools.reduce(lambda x, y: x + y, chi)
    chi_sum = jnp.sum(chi, axis=0, keepdims=True)
    live_sum = jnp.sum(cnt_v[...], axis=0, keepdims=True).astype(jnp.float32)
    stat_row = lax.broadcasted_iota(jnp.int32, (2, LANES), 0)
    mine = me_ra * n_dec + me_dec
    stat[mine] = jnp.where(stat_row == 0, chi_sum, live_sum)

    def share(target):
        pltpu.make_async_remote_copy(
            src_ref=stat.at[mine], dst_ref=stat.at[mine],
            send_sem=local_sem.at[3], recv_sem=stat_sem.at[0],
            device_id=target, device_id_type=MESH,
        ).start()

    pl.semaphore_wait(far_sem, n_dec - 1)
    everyone(share)

    def shared(sem):
        others = stat.at[pl.ds(0, n_ra * n_dec - 1)]
        pltpu.make_async_copy(others, others, sem).wait()

    lax.fori_loop(ends[1], chunks, lambda c, carry: accumulate(c * size, carry), 0)
    each(False, lambda way: await_bytes(halo_side(halo_col, way) if way else halo_ra, send_sem.at[way + 1]))
    lane, cell, first_tile, last_tile = position()

    def shift_dec(low, mid, high):
        up = turn(high, 1, 1)
        up_next = turn(up, cells_ra, 0)
        down = turn(low, -1, 1)
        down_next = turn(down, -cells_ra, 0)
        kept = (
            mid
            + jnp.where(lane == 0, jnp.where(first_tile, 0.0, up_next), up)
            + jnp.where(lane == LANES - 1, jnp.where(last_tile, 0.0, down_next), down)
        )
        return kept, up_next, down_next

    def pack_dec(packed, place, up_next, down_next):
        high = jnp.where((lane == place) & first_tile, turn(up_next, place, 1), packed[0])
        low = jnp.where((lane == place) & last_tile, turn(down_next, place + 1, 1), packed[1])
        return high, low

    edge = (zero, zero)
    corners = [(zero, zero), (zero, zero)]
    for group in range(groups):
        packed = [[zero] * 3, [zero] * 3]
        for term in range(group * cells_ra, min(TERMS, (group + 1) * cells_ra)):
            spot = term - group * cells_ra
            merged = []
            for at in range(3):
                down, mid, up = [bins[(3 * a + at) * TERMS + term] for a in range(3)]
                merged.append(
                    mid
                    + jnp.where(cell >= 1, turn(up, 1, 0), 0.0)
                    + jnp.where(cell <= cells_ra - 2, turn(down, -1, 0), 0.0)
                )
                packed[0][at] = jnp.where(cell == spot, turn(up, spot - (cells_ra - 1), 0), packed[0][at])
                packed[1][at] = jnp.where(cell == spot, turn(down, spot, 0), packed[1][at])
            kept, up_next, down_next = shift_dec(*merged)
            own[term] = kept
            edge = pack_dec(edge, term, up_next, down_next)
        for side in range(2):
            kept, up_next, down_next = shift_dec(*packed[side])
            send_ra[side, group] = kept
            corners[side] = pack_dec(corners[side], group, up_next, down_next)
    small = {
        (0, 1): edge[0], (0, -1): edge[1],
        (1, 1): corners[0][0], (1, -1): corners[0][1], (-1, 1): corners[1][0], (-1, -1): corners[1][1],
    }
    for place, step in enumerate(places):
        send_small[place] = small[step]

    def send_sums(way):
        if way == 0:
            for side, a in enumerate((1, -1)):
                remote(send_ra.at[side], recv_ra.at[side], sums_sem, 0, a)
        for place, (a, b) in enumerate(places):
            if b == way:
                remote(send_small.at[place], recv_small.at[place], sums_sem, way, a)

    def sums_side(ref, way):
        return ref.at[pl.ds(0 if way == 1 else 3, 3)]

    each(False, send_sums)
    each(True, lambda way: await_bytes(sums_side(recv_small, way) if way else recv_ra, sums_sem.at[way + 1]))
    received = {step: recv_small[place] for place, step in enumerate(places)}

    lane, cell, first_tile, last_tile = position()

    def unpack_dec(pair, place):
        high = jnp.where((lane == 0) & first_tile, turn(pair[0], -place, 1), 0.0)
        low = jnp.where((lane == LANES - 1) & last_tile, turn(pair[1], -(place + 1), 1), 0.0)
        return high + low

    edge = (received[0, 1], received[0, -1])
    total = []
    for group in range(groups):
        arrived = [
            recv_ra[side, group]
            + unpack_dec((received[a, 1], received[a, -1]), group)
            for side, a in enumerate((1, -1))
        ]
        for term in range(group * cells_ra, min(TERMS, (group + 1) * cells_ra)):
            spot = term - group * cells_ra
            total.append(
                own[term]
                + unpack_dec(edge, term)
                + jnp.where(cell == 0, turn(arrived[0], -spot, 0), 0.0)
                + jnp.where(cell == cells_ra - 1, turn(arrived[1], cells_ra - 1 - spot, 0), 0.0)
            )

    params = [p_v[p] for p in range(5)]
    lower = [[None] * 5 for _ in range(5)]
    inverse = [None] * 5
    forward = []
    for q in range(5):
        for p in range(q, 5):
            running = total[5 + PAIRS.index((q, p))]
            if p == q:
                running = running + 1.0
            for inner in range(q):
                running = running - lower[p][inner] * lower[q][inner]
            if p == q:
                inverse[q] = 1.0 / jnp.sqrt(running)
            else:
                lower[p][q] = running * inverse[q]
    for p in range(5):
        running = total[p] + params[p]
        for inner in range(p):
            running = running - lower[p][inner] * forward[inner]
        forward.append(running * inverse[p])
    answer = [None] * 5
    for p in range(4, -1, -1):
        running = forward[p]
        for inner in range(p + 1, 5):
            running = running - lower[inner][p] * answer[inner]
        answer[p] = running * inverse[p]
        out_ref[p] = answer[p]

    shared(stat_sem.at[0])
    stats = functools.reduce(lambda x, y: x + y, [stat[k] for k in range(n_ra * n_dec)])
    chi_ref[...] = jnp.full((8, LANES), jnp.sum(stats[0:1]) / jnp.sum(stats[1:2]))
    shared(local_sem.at[3])
    each(False, lambda way: await_bytes(sums_side(send_small, way) if way else send_ra, send_sem.at[way + 1]))


def per_device(n_ra, n_dec, design, observed, weight, params, offsets, counts):
    slots, cells_ra, cells_dec = observed.shape
    tiles = cells_dec // LANES
    rows = tiles * cells_ra

    def fold(x):
        x = x.reshape(x.shape[:-1] + (tiles, LANES))
        return jnp.swapaxes(x, -3, -2).reshape(x.shape[:-3] + (rows, LANES))

    chunks = next(c for c in (4, 2, 1) if slots % (2 * c) == 0)
    groups = -(-TERMS // cells_ra)
    anywhere = pl.BlockSpec(memory_space=pltpu.HBM)
    vmem = pl.BlockSpec(memory_space=pltpu.VMEM)
    new_params, chi = pl.pallas_call(
        functools.partial(kernel, n_ra, n_dec, cells_ra, chunks),
        out_shape=(
            jax.ShapeDtypeStruct((5, rows, LANES), jnp.float32),
            jax.ShapeDtypeStruct((8,128), jnp.float32),
        ),
        in_specs=[anywhere] * 6,
        out_specs=(vmem, vmem),
        scratch_shapes=[
            pltpu.VMEM((8, slots, rows, LANES), jnp.float32),
            pltpu.VMEM((slots, rows, LANES), jnp.int32),
            pltpu.VMEM((6, rows, LANES), jnp.float32),
            pltpu.VMEM((rows, LANES), jnp.int32),
            pltpu.VMEM((2, -(-5 // cells_ra), rows, LANES), jnp.float32),
            pltpu.VMEM((2, rows, LANES), jnp.float32),
            pltpu.VMEM((2, -(-5 // cells_ra), rows, LANES), jnp.float32),
            pltpu.VMEM((6, rows, LANES), jnp.float32),
            pltpu.VMEM((45, rows, LANES), jnp.float32),
            pltpu.VMEM((9 * TERMS, rows, LANES), jnp.float32),
            pltpu.VMEM((TERMS, rows, LANES), jnp.float32),
            pltpu.VMEM((2, groups, rows, LANES), jnp.float32),
            pltpu.VMEM((2, groups, rows, LANES), jnp.float32),
            pltpu.VMEM((6, rows, LANES), jnp.float32),
            pltpu.VMEM((6, rows, LANES), jnp.float32),
            pltpu.VMEM((n_ra * n_dec, 2, LANES), jnp.float32),
            pltpu.VMEM((3, rows, LANES), jnp.int32),
            pltpu.SemaphoreType.DMA((4,)),
            pltpu.SemaphoreType.DMA((1,)),
            pltpu.SemaphoreType.DMA((3,)),
            pltpu.SemaphoreType.DMA((3,)),
            pltpu.SemaphoreType.DMA((3,)),
            pltpu.SemaphoreType.DMA((1,)),
            pltpu.SemaphoreType.REGULAR,
        ],
        compiler_params=pltpu.CompilerParams(collective_id=0, has_side_effects=True, vmem_limit_bytes=16*1024*1024),
    )(*[pltpu.with_memory_space_constraint(fold(x), pltpu.HBM) for x in (design, observed, weight, params, offsets, counts)])
    def finish(x_ref, c_ref, out_ref, s_ref):
        out_ref[...] = x_ref[...]
        s_ref[0] = c_ref[0, 0]
    new_params, chi = pl.pallas_call(
        finish,
        out_shape=(
            jax.ShapeDtypeStruct((5, rows, LANES), jnp.float32),
            jax.ShapeDtypeStruct((1,), jnp.float32),
        ),
        in_specs=[vmem, vmem],
        out_specs=(vmem, pl.BlockSpec(memory_space=pltpu.SMEM)),
        compiler_params=pltpu.CompilerParams(vmem_limit_bytes=1024*1024),
    )(new_params, chi)
    new_params = jnp.swapaxes(new_params.reshape(5, tiles, cells_ra, LANES), 1, 2)
    return new_params.reshape(params.shape), chi[0]


def solution(mesh):
    return jax.shard_map(
        functools.partial(per_device, mesh.shape["ra"], mesh.shape["dec"]),
        mesh=mesh,
        in_specs=(
            P(None, None, "ra", "dec"),
            P(None, "ra", "dec"),
            P(None, "ra", "dec"),
            P(None, "ra", "dec"),
            P(None, "ra", "dec"),
            P("ra", "dec"),
        ),
        out_specs=(P(None, "ra", "dec"), P()),
        check_vma=False,
    )
```

time: 19.3 us -> 16.1 us (0.83)
  Pallas kernels: 18.5 us -> 15.3 us
    pallas_call x1, Pallas kernels: 17.9 us -> 14.7 us  [per_device(): pl.pallas_call(functools.partial(kernel, n_ra, n_dec, cells_ra, chunks),...]
where the time goes in v2:
time: 16.1 us; the launch traced here: 16 us
  Pallas kernels  15.3 us (95%)
  between operations  0.64 us (4%)
    pallas_call x1, Pallas kernels, per_device(): pl.pallas_call(functools.partial(kernel, n_ra, n_dec, cells_ra, chunks),...  14.7 us
    pallas_call x1, Pallas kernels, per_device(): pl.pallas_call(finish, out_shape=(jax.ShapeDtypeStruct((5, rows, LANES),...  0.62 us

profile of v2, /device:TPU:0, one launch (start us, length us, event | category | flops | bytes accessed | tf_op | source)
XLA Modules:
  0.0 16.0 jit_solution(4691208923569105581)
XLA Ops:
  0.6 14.7 %shard_map.77 = (f32[5,8,128]{2,1,0:T(8,128)S(1)}, f32[8,128]{1,0:T(8,128)S(1)}) custom-call(f32[5,80,8,128]{3,2,1,0:T(8,128)} %bitcast.36, f32[80,8,128]{2,1,0:T(8,128)} %bitcast.37, f32[80,8,128]{2,1,0:T(8,128)} %bitcast.38, f32[5,8,128]{2,1,0:T(8,128)} %bitcast.40, s32[80,8,128]{2,1,0:T(8,128)} %bitcast.39, s32[8,128]{1,0:T(8,128)} %bitcast.41), custom_call_target="tpu_custom_call" | custom-call | tf_op jit(solution)/shard_map/pallas_call | solution.py:435
  15.4 0.6 %shard_map.78 = (f32[5,8,128]{2,1,0:T(8,128)}, f32[1]{0:T(128)}) custom-call(f32[5,8,128]{2,1,0:T(8,128)S(1)} %get-tuple-element.6.x_ref, f32[8,128]{1,0:T(8,128)S(1)} %get-tuple-element.7.c_ref), custom_call_target="tpu_custom_call" | custom-call | tf_op jit(solution)/shard_map/pallas_call | solution.py:474

commit v3 on v2

--- a/solution.py
+++ b/solution.py
@@ -11,9 +11,9 @@
 PAIRS = [(p, q) for p in range(5) for q in range(p, 5)]
 TERMS = 5 + len(PAIRS)
 STEPS = (-1, 0, 1)
-GROUPS = (tuple(range(5, 15)), tuple(range(15, TERMS)) + tuple(range(5)))
 MESH = pl.DeviceIdType.MESH
-QUARTERS = (1, 3)
+EIGHTHS = (0, 7)
+RELAYS = (0, 2)
 WIDTH = 4
 
 
@@ -76,20 +76,20 @@
         pl.semaphore_signal(sem, inc=1, device_id=target, device_id_type=MESH)
 
     aside = sorted({1 % n_ra, -1 % n_ra} - {0})
-    lines = [(a, 0) for a in range(1, n_ra)] + [(0, b) for b in range(1, n_dec)]
-    corners_of = [(me_dec + b, [(a, b) for a in aside]) for b in (1, -1)]
+    line = [(a, 0) for a in range(1, n_ra)]
+    rows_of = [(me_dec + b, [(a, b) for a in (0, *aside)]) for b in (1, -1)]
     barrier = pltpu.get_barrier_semaphore()
-    greeted = len(lines)
-    for dec, peers in corners_of:
+    greeted = len(line)
+    for dec, peers in rows_of:
         inside = (dec >= 0) & (dec < n_dec)
-        greeted = greeted + len(aside) * inside.astype(jnp.int32)
+        greeted = greeted + len(peers) * inside.astype(jnp.int32)
 
         def greet(peers=peers):
             for peer in peers:
                 signal(barrier, device(*peer))
 
         pl.when(inside)(greet)
-    for peer in lines:
+    for peer in line:
         signal(barrier, device(*peer))
     for c in range(1, chunks):
         fetch(c)
@@ -112,52 +112,45 @@
 
     lax.fori_loop(0, 9 * TERMS, clear, 0, unroll=6)
     pltpu.make_async_copy(p_v, p_v, small_sem.at[0]).wait()
-    pairs = 2 if size % 4 == 0 else 1
-
-    def products(group, s, scale):
+
+    def products(s, scale):
         d = [design[p, s] for p in range(5)]
-        scaled = {}
-
-        def by(p):
-            if p not in scaled:
-                scaled[p] = scale * (observed[s] if p == 5 else d[p])
-            return scaled[p]
-
-        return [by(5) * d[term] if term < 5 else by(PAIRS[term - 5][0]) * d[PAIRS[term - 5][1]] for term in group]
-
-    def accumulate(begin, carry):
+        scaled = [scale * d[p] for p in range(5)]
+        return [scaled[p] * observed[s] for p in range(5)] + [scaled[p] * d[q] for p, q in PAIRS]
+
+    def accumulate(begin, count):
         def body(t, carry):
-            first = begin + 2 * pairs * t
-            codes, scales = [], []
-            for k in range(2 * pairs):
-                scale = jnp.where(first + k < cnt_v[...], weight[first + k], 0.0)
-                scales.append(scale)
-                codes.append(off_v[first + k])
-            same = [codes[2 * k] == codes[2 * k + 1] for k in range(pairs)]
-            for group in GROUPS:
-                values = [products(group, first + k, scales[k]) for k in range(2 * pairs)]
-                both = [
-                    [jnp.where(same[k], x + y, x) for x, y in zip(values[2 * k], values[2 * k + 1])]
-                    for k in range(pairs)
-                ]
-                for code in range(9):
-                    hits = [c == code for c in codes]
-                    for place, term in enumerate(group):
-                        total = bins[code * TERMS + term]
-                        for k in range(pairs):
-                            second = jnp.where(hits[2 * k + 1], values[2 * k + 1][place], 0.0)
-                            total = total + jnp.where(hits[2 * k], both[k][place], second)
-                        bins[code * TERMS + term] = total
+            slot = begin + 2 * t
+            codes = [off_v[slot], off_v[slot + 1]]
+            scales = [jnp.where(slot + k < cnt_v[...], weight[slot + k], 0.0) for k in range(2)]
+            first, second = [products(slot + k, scales[k]) for k in range(2)]
+            same = codes[0] == codes[1]
+            both = [jnp.where(same, x + y, x) for x, y in zip(first, second)]
+            for code in range(9):
+                hit, hit_second = codes[0] == code, codes[1] == code
+                for term in range(TERMS):
+                    value = jnp.where(hit, both[term], jnp.where(hit_second, second[term], 0.0))
+                    bins[code * TERMS + term] = bins[code * TERMS + term] + value
             return carry
 
-        return lax.fori_loop(0, size // (2 * pairs), body, carry)
-
-    def chunk(c, carry):
-        fetched(c)
-        return accumulate(c * size, carry)
-
-    ends = [-(-chunks * quarter // 4) for quarter in QUARTERS]
-    lax.fori_loop(0, ends[0], chunk, 0)
+        lax.fori_loop(0, count // 2, body, 0)
+
+    waited = set()
+
+    def span(begin, end, relays=()):
+        pieces = 0
+        for c in range(begin // size, -(-end // size)):
+            if c not in waited:
+                waited.add(c)
+                fetched(c)
+            first, last = max(begin, c * size), min(end, (c + 1) * size)
+            accumulate(first, last - first)
+            if pieces in relays and points:
+                relay(points.pop(0))
+            pieces += 1
+
+    cuts = [2 * (slots * eighth // 16) for eighth in EIGHTHS]
+    span(0, cuts[0])
 
     lane, cell, first_tile, last_tile = position()
     columns = [zero, zero]
@@ -195,6 +188,9 @@
     def await_bytes(ref, sem):
         pltpu.make_async_copy(ref, ref, sem).wait()
 
+    def edge_rows(b):
+        return pl.ds(0 if b == 1 else rows - cells_ra, cells_ra)
+
     def remote(source, target, sem, way, step_ra):
         pltpu.make_async_remote_copy(
             src_ref=source, dst_ref=target, send_sem=send_sem.at[way + 1], recv_sem=sem.at[way + 1],
@@ -210,17 +206,35 @@
             for side, a in enumerate((1, -1)):
                 remote(out_ra.at[side], halo_ra.at[side], halo_sem, 0, -a)
         for a, b in around.get(-way, []):
-            remote(out_col.at[0 if b == 1 else 1], halo_col.at[places.index((a, b))], halo_sem, way, -a)
+            rows_sent = edge_rows(b)
+            remote(out_col.at[0 if b == 1 else 1, rows_sent], halo_col.at[places.index((a, b)), rows_sent], halo_sem, way, -a)
 
     def halo_side(ref, way):
-        return ref.at[pl.ds(0 if way == -1 else 3, 3)]
+        return ref.at[pl.ds(0 if way == -1 else 3, 3), edge_rows(-way)]
 
     each(False, send_halo)
-    for b in range(1, n_dec):
-        signal(far_sem, device(0, b))
-    lax.fori_loop(ends[0], ends[1], chunk, 0)
-    for c in range(ends[1], chunks):
-        fetched(c)
+
+    def tell(b):
+        there = me_dec + b
+        pl.when((there >= 0) & (there < n_dec))(lambda: signal(far_sem.at[max(b, 0)], device(0, b)))
+
+    def hear(b):
+        pl.semaphore_wait(far_sem.at[max(b, 0)], 1)
+        tell(b)
+
+    def relay(point):
+        pl.when(me_dec == 1 + point)(lambda: hear(1))
+        pl.when(me_dec == n_dec - 2 - point)(lambda: hear(-1))
+
+    if n_dec > 1:
+        pl.when(me_dec == 0)(lambda: tell(1))
+        pl.when(me_dec == n_dec - 1)(lambda: tell(-1))
+    points = list(range(n_dec - 1))
+    span(cuts[0], cuts[1], RELAYS)
+    for c in range(chunks):
+        if c not in waited:
+            waited.add(c)
+            fetched(c)
     each(True, lambda way: await_bytes(halo_side(halo_col, way) if way else halo_ra, halo_sem.at[way + 1]))
     around = places
     lane, cell, first_tile, last_tile = position()
@@ -276,9 +290,10 @@
     chi = functools.reduce(lambda x, y: x + y, chi)
     chi_sum = jnp.sum(chi, axis=0, keepdims=True)
     live_sum = jnp.sum(cnt_v[...], axis=0, keepdims=True).astype(jnp.float32)
-    stat_row = lax.broadcasted_iota(jnp.int32, (2, LANES), 0)
+    half = lax.broadcasted_iota(jnp.int32, (1, LANES), 1) < LANES // 2
     mine = me_ra * n_dec + me_dec
-    stat[mine] = jnp.where(stat_row == 0, chi_sum, live_sum)
+    folded = jnp.where(half, chi_sum, live_sum) + turn(jnp.where(half, live_sum, chi_sum), LANES // 2, 1)
+    stat[mine] = folded
 
     def share(target):
         pltpu.make_async_remote_copy(
@@ -287,14 +302,15 @@
             device_id=target, device_id_type=MESH,
         ).start()
 
-    pl.semaphore_wait(far_sem, n_dec - 1)
+    while points:
+        relay(points.pop(0))
     everyone(share)
 
     def shared(sem):
         others = stat.at[pl.ds(0, n_ra * n_dec - 1)]
         pltpu.make_async_copy(others, others, sem).wait()
 
-    lax.fori_loop(ends[1], chunks, lambda c, carry: accumulate(c * size, carry), 0)
+    span(cuts[1], slots)
     each(False, lambda way: await_bytes(halo_side(halo_col, way) if way else halo_ra, send_sem.at[way + 1]))
     lane, cell, first_tile, last_tile = position()
 
@@ -351,10 +367,10 @@
                 remote(send_ra.at[side], recv_ra.at[side], sums_sem, 0, a)
         for place, (a, b) in enumerate(places):
             if b == way:
-                remote(send_small.at[place], recv_small.at[place], sums_sem, way, a)
+                remote(send_small.at[place, edge_rows(b)], recv_small.at[place, edge_rows(b)], sums_sem, way, a)
 
     def sums_side(ref, way):
-        return ref.at[pl.ds(0 if way == 1 else 3, 3)]
+        return ref.at[pl.ds(0 if way == 1 else 3, 3), edge_rows(way)]
 
     each(False, send_sums)
     each(True, lambda way: await_bytes(sums_side(recv_small, way) if way else recv_ra, sums_sem.at[way + 1]))
@@ -412,11 +428,13 @@
         answer[p] = running * inverse[p]
         out_ref[p] = answer[p]
 
+    shared(local_sem.at[3])
+    each(False, lambda way: await_bytes(sums_side(send_small, way) if way else send_ra, send_sem.at[way + 1]))
     shared(stat_sem.at[0])
     stats = functools.reduce(lambda x, y: x + y, [stat[k] for k in range(n_ra * n_dec)])
-    chi_ref[...] = jnp.full((8, LANES), jnp.sum(stats[0:1]) / jnp.sum(stats[1:2]))
-    shared(local_sem.at[3])
-    each(False, lambda way: await_bytes(sums_side(send_small, way) if way else send_ra, send_sem.at[way + 1]))
+    chi_sum = jnp.sum(jnp.where(half, stats, 0.0), axis=1, keepdims=True)
+    live_sum = jnp.sum(jnp.where(half, 0.0, stats), axis=1, keepdims=True)
+    chi_ref[0:1] = jnp.broadcast_to(chi_sum / live_sum, (1, LANES))
 
 
 def per_device(n_ra, n_dec, design, observed, weight, params, offsets, counts):
@@ -456,7 +474,7 @@
             pltpu.VMEM((2, groups, rows, LANES), jnp.float32),
             pltpu.VMEM((6, rows, LANES), jnp.float32),
             pltpu.VMEM((6, rows, LANES), jnp.float32),
-            pltpu.VMEM((n_ra * n_dec, 2, LANES), jnp.float32),
+            pltpu.VMEM((n_ra * n_dec, 1, LANES), jnp.float32),
             pltpu.VMEM((3, rows, LANES), jnp.int32),
             pltpu.SemaphoreType.DMA((4,)),
             pltpu.SemaphoreType.DMA((1,)),
@@ -464,7 +482,7 @@
             pltpu.SemaphoreType.DMA((3,)),
             pltpu.SemaphoreType.DMA((3,)),
             pltpu.SemaphoreType.DMA((1,)),
-            pltpu.SemaphoreType.REGULAR,
+            pltpu.SemaphoreType.REGULAR((2,)),
         ],
         compiler_params=pltpu.CompilerParams(collective_id=0, has_side_effects=True, vmem_limit_bytes=16*1024*1024),
     )(*[pltpu.with_memory_space_constraint(fold(x), pltpu.HBM) for x in (design, observed, weight, params, offsets, counts)])

time: 16.1 us -> 15.5 us (0.963)
  Pallas kernels: 15.3 us -> 14.7 us
    pallas_call x1, Pallas kernels: 14.7 us -> 14.1 us  [per_device(): pl.pallas_call(functools.partial(kernel, n_ra, n_dec, cells_ra, chunks),...]
where the time goes in v3:
time: 15.5 us; the launch traced here: 15.4 us
  Pallas kernels  14.7 us (95%)
  between operations  0.64 us (4%)
    pallas_call x1, Pallas kernels, per_device(): pl.pallas_call(functools.partial(kernel, n_ra, n_dec, cells_ra, chunks),...  14.1 us
    pallas_call x1, Pallas kernels, per_device(): pl.pallas_call(finish, out_shape=(jax.ShapeDtypeStruct((5, rows, LANES),...  0.62 us

profile of v3, /device:TPU:0, one launch (start us, length us, event | category | flops | bytes accessed | tf_op | source)
XLA Modules:
  0.0 15.4 jit_solution(14205117740993599151)
XLA Ops:
  0.6 14.1 %shard_map.77 = (f32[5,8,128]{2,1,0:T(8,128)S(1)}, f32[8,128]{1,0:T(8,128)S(1)}) custom-call(f32[5,80,8,128]{3,2,1,0:T(8,128)} %bitcast.36, f32[80,8,128]{2,1,0:T(8,128)} %bitcast.37, f32[80,8,128]{2,1,0:T(8,128)} %bitcast.38, f32[5,8,128]{2,1,0:T(8,128)} %bitcast.40, s32[80,8,128]{2,1,0:T(8,128)} %bitcast.39, s32[8,128]{1,0:T(8,128)} %bitcast.41), custom_call_target="tpu_custom_call" | custom-call | tf_op jit(solution)/shard_map/pallas_call | solution.py:453
  14.7 0.6 %shard_map.78 = (f32[5,8,128]{2,1,0:T(8,128)}, f32[1]{0:T(128)}) custom-call(f32[5,8,128]{2,1,0:T(8,128)S(1)} %get-tuple-element.6.x_ref, f32[8,128]{1,0:T(8,128)S(1)} %get-tuple-element.7.c_ref), custom_call_target="tpu_custom_call" | custom-call | tf_op jit(solution)/shard_map/pallas_call | solution.py:492

commit v4 on v3

--- a/solution.py
+++ b/solution.py
@@ -12,8 +12,8 @@
 TERMS = 5 + len(PAIRS)
 STEPS = (-1, 0, 1)
 MESH = pl.DeviceIdType.MESH
-EIGHTHS = (0, 7)
-RELAYS = (0, 2)
+PARTS = (0, 35)
+RELAYS = (1, 2)
 WIDTH = 4
 
 
@@ -149,7 +149,7 @@
                 relay(points.pop(0))
             pieces += 1
 
-    cuts = [2 * (slots * eighth // 16) for eighth in EIGHTHS]
+    cuts = [2 * (slots * part // 80) for part in PARTS]
     span(0, cuts[0])
 
     lane, cell, first_tile, last_tile = position()
@@ -177,9 +177,9 @@
         for place in range(3, 6):
             recv_small[place] = zero
 
-    def each(arrives, action):
+    def each(action):
         for way in STEPS:
-            there = me_dec - way if arrives else me_dec + way
+            there = me_dec + way
             if way == 0:
                 action(way)
             else:
@@ -193,7 +193,7 @@
 
     def remote(source, target, sem, way, step_ra):
         pltpu.make_async_remote_copy(
-            src_ref=source, dst_ref=target, send_sem=send_sem.at[way + 1], recv_sem=sem.at[way + 1],
+            src_ref=source, dst_ref=target, send_sem=send_sem.at[0], recv_sem=sem.at[0],
             device_id=device(step_ra, way), device_id_type=MESH,
         ).start()
 
@@ -209,10 +209,14 @@
             rows_sent = edge_rows(b)
             remote(out_col.at[0 if b == 1 else 1, rows_sent], halo_col.at[places.index((a, b)), rows_sent], halo_sem, way, -a)
 
-    def halo_side(ref, way):
-        return ref.at[pl.ds(0 if way == -1 else 3, 3), edge_rows(-way)]
-
-    each(False, send_halo)
+    def await_all(planes, sem):
+        sides = (me_dec > 0).astype(jnp.int32) + (me_dec < n_dec - 1).astype(jnp.int32)
+        for count in range(0 if n_dec == 1 else 1, min(n_dec, 3)):
+            size_of = bins.at[pl.ds(0, planes * tiles + 3 * count), pl.ds(0, cells_ra)]
+            pl.when(sides == count)(lambda size_of=size_of: await_bytes(size_of, sem.at[0]))
+
+    halo_planes, sums_planes = 2 * halo_ra.shape[1], 2 * groups
+    each(send_halo)
 
     def tell(b):
         there = me_dec + b
@@ -235,7 +239,7 @@
         if c not in waited:
             waited.add(c)
             fetched(c)
-    each(True, lambda way: await_bytes(halo_side(halo_col, way) if way else halo_ra, halo_sem.at[way + 1]))
+    await_all(halo_planes, halo_sem)
     around = places
     lane, cell, first_tile, last_tile = position()
 
@@ -311,7 +315,7 @@
         pltpu.make_async_copy(others, others, sem).wait()
 
     span(cuts[1], slots)
-    each(False, lambda way: await_bytes(halo_side(halo_col, way) if way else halo_ra, send_sem.at[way + 1]))
+    await_all(halo_planes, send_sem)
     lane, cell, first_tile, last_tile = position()
 
     def shift_dec(low, mid, high):
@@ -369,11 +373,8 @@
             if b == way:
                 remote(send_small.at[place, edge_rows(b)], recv_small.at[place, edge_rows(b)], sums_sem, way, a)
 
-    def sums_side(ref, way):
-        return ref.at[pl.ds(0 if way == 1 else 3, 3), edge_rows(way)]
-
-    each(False, send_sums)
-    each(True, lambda way: await_bytes(sums_side(recv_small, way) if way else recv_ra, sums_sem.at[way + 1]))
+    each(send_sums)
+    await_all(sums_planes, sums_sem)
     received = {step: recv_small[place] for place, step in enumerate(places)}
 
     lane, cell, first_tile, last_tile = position()
@@ -429,7 +430,7 @@
         out_ref[p] = answer[p]
 
     shared(local_sem.at[3])
-    each(False, lambda way: await_bytes(sums_side(send_small, way) if way else send_ra, send_sem.at[way + 1]))
+    await_all(sums_planes, send_sem)
     shared(stat_sem.at[0])
     stats = functools.reduce(lambda x, y: x + y, [stat[k] for k in range(n_ra * n_dec)])
     chi_sum = jnp.sum(jnp.where(half, stats, 0.0), axis=1, keepdims=True)
@@ -478,9 +479,9 @@
             pltpu.VMEM((3, rows, LANES), jnp.int32),
             pltpu.SemaphoreType.DMA((4,)),
             pltpu.SemaphoreType.DMA((1,)),
-            pltpu.SemaphoreType.DMA((3,)),
-            pltpu.SemaphoreType.DMA((3,)),
-            pltpu.SemaphoreType.DMA((3,)),
+            pltpu.SemaphoreType.DMA((1,)),
+            pltpu.SemaphoreType.DMA((1,)),
+            pltpu.SemaphoreType.DMA((1,)),
             pltpu.SemaphoreType.DMA((1,)),
             pltpu.SemaphoreType.REGULAR((2,)),
         ],
@@ -488,19 +489,19 @@
     )(*[pltpu.with_memory_space_constraint(fold(x), pltpu.HBM) for x in (design, observed, weight, params, offsets, counts)])
     def finish(x_ref, c_ref, out_ref, s_ref):
         out_ref[...] = x_ref[...]
-        s_ref[0] = c_ref[0, 0]
+        s_ref[...] = c_ref[0:1, 0:1]
     new_params, chi = pl.pallas_call(
         finish,
         out_shape=(
             jax.ShapeDtypeStruct((5, rows, LANES), jnp.float32),
-            jax.ShapeDtypeStruct((1,), jnp.float32),
+            jax.ShapeDtypeStruct((1, 1), jnp.float32),
         ),
         in_specs=[vmem, vmem],
-        out_specs=(vmem, pl.BlockSpec(memory_space=pltpu.SMEM)),
+        out_specs=(vmem, vmem),
         compiler_params=pltpu.CompilerParams(vmem_limit_bytes=1024*1024),
     )(new_params, chi)
     new_params = jnp.swapaxes(new_params.reshape(5, tiles, cells_ra, LANES), 1, 2)
-    return new_params.reshape(params.shape), chi[0]
+    return new_params.reshape(params.shape), chi[0, 0]
 
 
 def solution(mesh):

time: 15.5 us -> 15.5 us (level)
  no operation moved by 1% of the time
where the time goes in v4:
time: 15.5 us; the launch traced here: 15.3 us
  Pallas kernels  14.7 us (95%)
  between operations  0.64 us (4%)
    pallas_call x1, Pallas kernels, per_device(): pl.pallas_call(functools.partial(kernel, n_ra, n_dec, cells_ra, chunks),...  14.1 us
    pallas_call x1, Pallas kernels, per_device(): pl.pallas_call(finish, out_shape=(jax.ShapeDtypeStruct((5, rows, LANES),...  0.61 us

profile of v4, /device:TPU:0, one launch (start us, length us, event | category | flops | bytes accessed | tf_op | source)
XLA Modules:
  0.0 15.3 jit_solution(2245949868545499490)
XLA Ops:
  0.6 14.1 %shard_map.77 = (f32[5,8,128]{2,1,0:T(8,128)S(1)}, f32[8,128]{1,0:T(8,128)S(1)}) custom-call(f32[5,80,8,128]{3,2,1,0:T(8,128)} %bitcast.36, f32[80,8,128]{2,1,0:T(8,128)} %bitcast.37, f32[80,8,128]{2,1,0:T(8,128)} %bitcast.38, f32[5,8,128]{2,1,0:T(8,128)} %bitcast.40, s32[80,8,128]{2,1,0:T(8,128)} %bitcast.39, s32[8,128]{1,0:T(8,128)} %bitcast.41), custom_call_target="tpu_custom_call" | custom-call | tf_op jit(solution)/shard_map/pallas_call | solution.py:454
  14.7 0.6 %shard_map.78 = (f32[5,8,128]{2,1,0:T(8,128)}, f32[1,1]{1,0:T(1,128)}) custom-call(f32[5,8,128]{2,1,0:T(8,128)S(1)} %get-tuple-element.6.x_ref, f32[8,128]{1,0:T(8,128)S(1)} %get-tuple-element.7.c_ref), custom_call_target="tpu_custom_call" | custom-call | tf_op jit(solution)/shard_map/pallas_call | solution.py:493

commit v5 on v4

--- a/solution.py
+++ b/solution.py
@@ -52,10 +52,6 @@
         part = data.at[:, pl.ds(c * size, size)]
         pltpu.make_async_copy(part, part, local_sem.at[c]).wait()
 
-    pltpu.make_async_copy(cnt_hbm, cnt_v, small_sem.at[0]).start()
-    pltpu.make_async_copy(p_hbm, p_v.at[pl.ds(0, 5)], small_sem.at[0]).start()
-    fetch(0)
-
     def device(step_ra, step_dec):
         return (lax.rem(me_ra + step_ra + n_ra, n_ra), lax.rem(me_dec + step_dec + n_dec, n_dec))
 
@@ -89,6 +85,9 @@
                 signal(barrier, device(*peer))
 
         pl.when(inside)(greet)
+    pltpu.make_async_copy(cnt_hbm, cnt_v, small_sem.at[0]).start()
+    pltpu.make_async_copy(p_hbm, p_v.at[pl.ds(0, 5)], small_sem.at[0]).start()
+    fetch(0)
     for peer in line:
         signal(barrier, device(*peer))
     for c in range(1, chunks):

time: 15.5 us -> 15.5 us (level)
  no operation moved by 1% of the time
where the time goes in v5:
time: 15.5 us; the launch traced here: 15.4 us
  Pallas kernels  14.7 us (95%)
  between operations  0.64 us (4%)
    pallas_call x1, Pallas kernels, per_device(): pl.pallas_call(functools.partial(kernel, n_ra, n_dec, cells_ra, chunks),...  14.1 us
    pallas_call x1, Pallas kernels, per_device(): pl.pallas_call(finish, out_shape=(jax.ShapeDtypeStruct((5, rows, LANES),...  0.61 us

profile of v5, /device:TPU:0, one launch (start us, length us, event | category | flops | bytes accessed | tf_op | source)
XLA Modules:
  0.0 15.4 jit_solution(12361109138156417353)
XLA Ops:
  0.6 14.1 %shard_map.77 = (f32[5,8,128]{2,1,0:T(8,128)S(1)}, f32[8,128]{1,0:T(8,128)S(1)}) custom-call(f32[5,80,8,128]{3,2,1,0:T(8,128)} %bitcast.36, f32[80,8,128]{2,1,0:T(8,128)} %bitcast.37, f32[80,8,128]{2,1,0:T(8,128)} %bitcast.38, f32[5,8,128]{2,1,0:T(8,128)} %bitcast.40, s32[80,8,128]{2,1,0:T(8,128)} %bitcast.39, s32[8,128]{1,0:T(8,128)} %bitcast.41), custom_call_target="tpu_custom_call" | custom-call | tf_op jit(solution)/shard_map/pallas_call | solution.py:453
  14.8 0.6 %shard_map.78 = (f32[5,8,128]{2,1,0:T(8,128)}, f32[1,1]{1,0:T(1,128)}) custom-call(f32[5,8,128]{2,1,0:T(8,128)S(1)} %get-tuple-element.6.x_ref, f32[8,128]{1,0:T(8,128)S(1)} %get-tuple-element.7.c_ref), custom_call_target="tpu_custom_call" | custom-call | tf_op jit(solution)/shard_map/pallas_call | solution.py:492
